TPU v7x, 32 devices: a whole 2x2x4 slice. The times are simulated.
32 devices in a mesh: dp: 8 (over z, x), expert: 4 (over y, core).
Axes of the slice: x: 2, y: 2, z: 4, core: 2. Of those that a mesh axis runs over, the one named last changes fastest.
Arguments:
- tokens: bfloat16 [4096, 2048], P(('dp', 'expert')), may hold values from -6 to 6
- expert_ids: int32 [4096, 8], P(('dp', 'expert')), may hold values from 0 to 15, all different within a row
- route_probs: float32 [4096, 8], P(('dp', 'expert')), may hold values from 0.05 to 1
- shard_limit: int32 [32, 16], P(('dp', 'expert')), may hold values from 32 to 64
- gate_proj: bfloat16 [32, 2048, 384], P(('dp', 'expert')), may hold values from -0.125 to 0.125
- up_proj: bfloat16 [32, 2048, 384], P(('dp', 'expert')), may hold values from -0.125 to 0.125
- down_proj: bfloat16 [32, 384, 2048], P(('dp', 'expert')), may hold values from -0.21875 to 0.21875
Outputs:
- mixed_out: bfloat16 [4096, 2048], P(('dp', 'expert'))
Inputs may be any that keep to these rules, and one draw needn't show every extreme that they name: `expert_ids`: each row names 8 different experts.
All inputs are finite; a program needn't handle non-finite values.
Results may differ from a plain program's by a relative error of at most 0.0095.
Values may be sent and summed in bfloat16 or wider, within the bound.
A program may use at most 64 MiB of HBM per device.

v0:
```python
import functools

import jax
import jax.numpy as jnp
from jax import lax
from jax.experimental import pallas as pl
from jax.experimental.pallas import tpu as pltpu
from jax.sharding import PartitionSpec as P

BF = jnp.bfloat16
F32 = jnp.float32
SIXTEENTHS = (10, 6)


class Wires:
    def __init__(self, ssem, rsem):
        self.ssem, self.rsem = ssem, rsem
        self.count = 0
        self.sent = []

    def lane(self):
        self.count += 1
        return self.count - 1

    def copy(self, src, dst, lane, to):
        return pltpu.make_async_remote_copy(
            src_ref=src,
            dst_ref=dst,
            send_sem=self.ssem.at[lane],
            recv_sem=self.rsem.at[lane],
            device_id={"dp": to},
            device_id_type=pl.DeviceIdType.MESH,
        )

    def send(self, src, dst, lane, to):
        moved = self.copy(src, dst, lane, to)
        moved.start()
        self.sent.append(moved)

    def arrive(self, dst, lane, to):
        self.copy(dst, dst, lane, to).wait_recv()

    def finish(self):
        for moved in self.sent:
            moved.wait_send()


def places(ring):
    me = lax.axis_index("dp")
    z, x = lax.div(me, 2), lax.rem(me, 2)
    ahead = lax.rem(z + 1, ring) * 2 + x
    behind = lax.rem(z + ring - 1, ring) * 2 + x
    return z, x, ahead, behind, z * 2 + 1 - x


def pieces(rows):
    unit = rows // 8
    return [(0, 3 * unit), (3 * unit, 3 * unit), (6 * unit, unit), (7 * unit, unit)]


def greet(peers):
    barrier = pltpu.get_barrier_semaphore()
    for peer in peers:
        pl.semaphore_signal(
            barrier, inc=1, device_id={"dp": peer}, device_id_type=pl.DeviceIdType.MESH
        )
    pl.semaphore_wait(barrier, len(peers))


def gather_kernel(ring, src, out, ssem, rsem, own_sem):
    z, x, ahead, behind, other = places(ring)
    greet((ahead, behind, other))
    rows = src.shape[0]
    spans = pieces(rows)
    wires = Wires(ssem, rsem)
    to = [ahead, behind]

    def at(zz, xx, k):
        begin, count = spans[k]
        start = pl.multiple_of((zz * 2 + xx) * rows + begin, rows // 8)
        return out.at[pl.ds(start, count)]

    def back(k, s):
        return lax.rem(z + (ring - s if k % 2 == 0 else s), ring)

    own = [src.at[pl.ds(*spans[k])] for k in range(4)]
    ring_lane = {}
    for k in range(4):
        for s in range(ring - 1):
            ring_lane[k, 0, s] = wires.lane()
            if k >= 2:
                ring_lane[k, 1, s] = wires.lane()
    cross_lane = {}
    for k in range(4):
        for s in range(ring if k < 2 else 1):
            cross_lane[k, s] = wires.lane()

    for k in (2, 3):
        wires.send(own[k], at(z, x, k), cross_lane[k, 0], other)
    for k in range(4):
        wires.send(own[k], at(z, x, k), ring_lane[k, 0, 0], to[k % 2])
    for k in (0, 1):
        wires.send(own[k], at(z, x, k), cross_lane[k, 0], other)
    local = pltpu.make_async_copy(
        src, out.at[pl.ds(pl.multiple_of((z * 2 + x) * rows, rows), rows)], own_sem
    )
    local.start()
    for k in (2, 3):
        block = at(z, 1 - x, k)
        wires.arrive(block, cross_lane[k, 0], other)
        wires.send(block, block, ring_lane[k, 1, 0], to[k % 2])
    for s in range(ring - 1):
        for k in (0, 1):
            block = at(back(k, s + 1), x, k)
            wires.arrive(block, ring_lane[k, 0, s], other)
            if s < ring - 2:
                wires.send(block, block, ring_lane[k, 0, s + 1], to[k % 2])
            wires.send(block, block, cross_lane[k, s + 1], other)
        for j in range(2):
            for k in (2, 3):
                block = at(back(k, s + 1), x if j == 0 else 1 - x, k)
                wires.arrive(block, ring_lane[k, j, s], other)
                if s < ring - 2:
                    wires.send(block, block, ring_lane[k, j, s + 1], to[k % 2])
    for s in range(ring):
        for k in (0, 1):
            wires.arrive(at(back(k, s), 1 - x, k), cross_lane[k, s], other)
    local.wait()
    wires.finish()


def scatter_kernel(ring, part, out, cross_a, ring_a, ring_b, cross_b, ssem, rsem):
    z, x, ahead, behind, other = places(ring)
    greet((ahead, behind, other))
    rows = out.shape[0]
    spans = pieces(rows)
    wires = Wires(ssem, rsem)
    to = [ahead, behind]

    def at(zz, xx, k):
        begin, count = spans[k]
        start = pl.multiple_of((zz * 2 + xx) * rows + begin, rows // 8)
        return part.at[pl.ds(start, count)]

    def goal(k, s):
        return lax.rem(z + (ring - 1 - s if k % 2 == 0 else 1 + s), ring)

    def total(*refs):
        value = refs[0][...].astype(F32)
        for ref in refs[1:]:
            value = value + ref[...].astype(F32)
        return value.astype(BF)

    lanes = {}
    for k in range(4):
        for s in range(ring - 1):
            lanes[k, 0, s] = wires.lane()
            if k >= 2:
                lanes[k, 1, s] = wires.lane()
        for s in range(ring if k < 2 else 1):
            lanes["c", k, s] = wires.lane()

    for j in range(2):
        for k in (2, 3):
            wires.send(
                at(goal(k, 0), x if j == 0 else 1 - x, k),
                ring_b.at[k - 2, j, 0],
                lanes[k, j, 0],
                to[k % 2],
            )
    for s in range(ring):
        for k in (0, 1):
            wires.send(
                at(goal(k, s), 1 - x, k), cross_a.at[k, s], lanes["c", k, s], other
            )
    for s in range(ring - 1):
        for k in (0, 1):
            mine = cross_a.at[k, s]
            wires.arrive(mine, lanes["c", k, s], other)
            terms = [mine, at(goal(k, s), x, k)]
            if s > 0:
                came = ring_a.at[k, s - 1]
                wires.arrive(came, lanes[k, 0, s - 1], other)
                terms.append(came)
            mine[...] = total(*terms)
            wires.send(mine, ring_a.at[k, s], lanes[k, 0, s], to[k % 2])
        if s > 0:
            for j in (1, 0):
                for k in (2, 3):
                    came = ring_b.at[k - 2, j, s - 1]
                    wires.arrive(came, lanes[k, j, s - 1], other)
                    came[...] = total(came, at(goal(k, s), x if j == 0 else 1 - x, k))
                    wires.send(came, ring_b.at[k - 2, j, s], lanes[k, j, s], to[k % 2])
    for k in (2, 3):
        came = ring_b.at[k - 2, 1, ring - 2]
        wires.arrive(came, lanes[k, 1, ring - 2], other)
        came[...] = total(came, at(z, 1 - x, k))
        wires.send(came, cross_b.at[k - 2], lanes["c", k, 0], other)
    for k in (0, 1):
        wires.arrive(cross_a.at[k, ring - 1], lanes["c", k, ring - 1], other)
        wires.arrive(ring_a.at[k, ring - 2], lanes[k, 0, ring - 2], other)
        out[pl.ds(*spans[k])] = total(
            at(z, x, k), cross_a.at[k, ring - 1], ring_a.at[k, ring - 2]
        )
    for k in (2, 3):
        came = ring_b.at[k - 2, 0, ring - 2]
        wires.arrive(came, lanes[k, 0, ring - 2], other)
        wires.arrive(cross_b.at[k - 2], lanes["c", k, 0], other)
        out[pl.ds(*spans[k])] = total(at(z, x, k), came, cross_b.at[k - 2])
    wires.finish()


def kernel_params(number):
    return pltpu.CompilerParams(
        collective_id=number, has_side_effects=True, vmem_limit_bytes=48 << 20
    )


VM = pl.BlockSpec(memory_space=pltpu.VMEM)


def gather_dp(block, number):
    dp_size = lax.axis_size("dp")
    ring = dp_size // 2
    count = 8 * ring - 4
    return pl.pallas_call(
        functools.partial(gather_kernel, ring),
        name="gather%d" % number,
        out_shape=jax.ShapeDtypeStruct((dp_size * block.shape[0], block.shape[1]), block.dtype),
        in_specs=[VM],
        out_specs=VM,
        scratch_shapes=[
            pltpu.SemaphoreType.DMA((count,)),
            pltpu.SemaphoreType.DMA((count,)),
            pltpu.SemaphoreType.DMA,
        ],
        compiler_params=kernel_params(number),
        cost_estimate=pl.CostEstimate(flops=0, transcendentals=0, bytes_accessed=60 << 20),
    )(block)


def scatter_dp(parts, number):
    dp_size = lax.axis_size("dp")
    ring = dp_size // 2
    rows, wide = parts.shape[0] // dp_size, parts.shape[1]
    (_, long), (_, short) = pieces(rows)[1:3]
    count = 8 * ring - 4
    return pl.pallas_call(
        functools.partial(scatter_kernel, ring),
        name="scatter%d" % number,
        out_shape=jax.ShapeDtypeStruct((rows, wide), parts.dtype),
        in_specs=[VM],
        out_specs=VM,
        scratch_shapes=[
            pltpu.VMEM((2, ring, long, wide), BF),
            pltpu.VMEM((2, ring - 1, long, wide), BF),
            pltpu.VMEM((2, 2, ring - 1, short, wide), BF),
            pltpu.VMEM((2, short, wide), BF),
            pltpu.SemaphoreType.DMA((count,)),
            pltpu.SemaphoreType.DMA((count,)),
        ],
        compiler_params=kernel_params(number),
        cost_estimate=pl.CostEstimate(flops=0, transcendentals=0, bytes_accessed=60 << 20),
    )(parts)


def swap_cores(block, col_size):
    return lax.ppermute(block, "expert", [(c, c ^ 1) for c in range(col_size)])


def turn(block, col_size, by):
    route = [(c, (c + 2 * by) % col_size) for c in range(col_size)]
    return lax.ppermute(block, "expert", route)


def slot_matrices(ids, probs, limits, col_cap, per_row):
    dp_size, tok_rows, _ = ids.shape
    count_y = per_row
    first = lax.axis_index("dp") * per_row
    here = lax.axis_index("expert") // 2
    wanted = first + lax.rem(here + jnp.arange(count_y, dtype=jnp.int32), count_y)
    match = ids[None] == wanted.astype(F32)[:, None, None, None]
    chosen = jnp.sum(match.astype(F32), axis=3)
    weight = jnp.sum(jnp.where(match, probs[None], 0.0), axis=3)
    lower = (jnp.arange(tok_rows)[:, None] < jnp.arange(tok_rows)[None, :]).astype(BF)
    rank = jnp.dot(
        chosen.reshape(-1, tok_rows).astype(BF), lower, preferred_element_type=F32
    ).reshape(chosen.shape)
    pick = (jnp.arange(limits.shape[1], dtype=jnp.int32)[None, :] == wanted[:, None]).astype(F32)
    limit = jnp.sum(pick[:, None, :] * limits[None], axis=2)
    kept = jnp.minimum(jnp.sum(chosen, axis=2), limit)
    earlier = (jnp.arange(dp_size)[:, None] < jnp.arange(dp_size)[None, :]).astype(F32)
    offset = jnp.sum(kept[:, :, None] * earlier[None], axis=1)
    slot = offset[:, :, None] + rank
    keep = (chosen > 0) & (rank < limit[:, :, None]) & (slot < col_cap)
    slot = jnp.where(keep, slot, float(col_cap)).astype(jnp.int32).reshape(count_y, 1, -1)
    weight = weight.reshape(count_y, 1, -1)
    spot = jnp.arange(col_cap, dtype=jnp.int32)[None, :, None] == slot
    return spot.astype(BF), jnp.where(spot, weight, 0.0).astype(BF)


def on_device(tokens, expert_ids, route_probs, shard_limit, gate_proj, up_proj, down_proj):
    tok_rows, width = tokens.shape
    top = expert_ids.shape[1]
    experts = shard_limit.shape[1]
    dp_size = lax.axis_size("dp")
    col_size = lax.axis_size("expert")
    per_row = col_size // 2
    capacity = tok_rows * top // experts
    col_cap = dp_size * capacity // 2
    bounds = [0]
    for share in SIXTEENTHS:
        bounds.append(bounds[-1] + width * share // 16)
    spans = list(zip(bounds[:-1], bounds[1:]))
    part = bounds[1]

    used = 2 * top + experts
    meta = jnp.concatenate(
        [
            expert_ids.astype(BF),
            route_probs.astype(BF),
            jnp.broadcast_to(shard_limit.astype(BF), (tok_rows, experts)),
            jnp.zeros((tok_rows, -used % 128), BF),
        ],
        axis=1,
    )
    first = gather_dp(jnp.concatenate([tokens[:, :part], meta], axis=1), 0)
    columns = [first]
    for n, (low, high) in enumerate(spans[1:], 1):
        block, columns[-1] = lax.optimization_barrier((tokens[:, low:high], columns[-1]))
        columns.append(gather_dp(block, 2 * n))
    first = columns[0]
    columns[0] = first[:, :part]
    info = first[:, part:].reshape(dp_size, tok_rows, -1).astype(F32)
    spots, weights = slot_matrices(
        info[:, :, :top],
        info[:, :, top : 2 * top],
        info[:, 0, 2 * top : used],
        col_cap,
        per_row,
    )

    gate_half, up_half, down_half = gate_proj[0], up_proj[0], down_proj[0]
    stacks = []
    for n in range(len(spans)):
        slots = jnp.einsum("rst,td->rsd", spots, columns[n], preferred_element_type=F32).astype(BF)
        held = [slots[0]] + [turn(slots[r], col_size, r) for r in range(1, per_row)]
        held = jnp.concatenate(held, axis=0)
        stacks.append(jnp.concatenate([held, swap_cores(held, col_size)], axis=0))
    rows = jnp.concatenate(stacks, axis=1)
    gate_val = jnp.dot(rows, gate_half, preferred_element_type=F32)
    up_val = jnp.dot(rows, up_half, preferred_element_type=F32)
    hidden = (jax.nn.silu(gate_val) * up_val).astype(BF)

    own = per_row * col_cap
    homes = []
    for low, high in spans[::-1]:
        partial = jnp.dot(hidden, down_half[:, low:high], preferred_element_type=F32).astype(BF)
        back = swap_cores(partial[own:], col_size)
        merged = (partial[:own].astype(F32) + back.astype(F32)).astype(BF)
        if not homes:
            hidden, merged = lax.optimization_barrier((hidden, merged))
        merged = merged.reshape(per_row, col_cap, high - low)
        home = [merged[0]] + [turn(merged[r], col_size, -r) for r in range(1, per_row)]
        homes.append(jnp.stack(home, axis=0))
    outs = []
    for n, home in enumerate(homes):
        if outs:
            home, outs[-1] = lax.optimization_barrier((home, outs[-1]))
        mixed = jnp.einsum("rst,rsd->td", weights, home, preferred_element_type=F32).astype(BF)
        outs.append(scatter_dp(mixed, 2 * n + 1))
    return jnp.concatenate(outs[::-1], axis=1)


def solution(mesh):
    rows = P(("dp", "expert"), None)
    blocks = P(("dp", "expert"), None, None)
    return jax.shard_map(
        on_device,
        mesh=mesh,
        in_specs=(rows, rows, rows, rows, blocks, blocks, blocks),
        out_specs=rows,
        check_vma=False,
    )
```

profile of v0, /device:TPU:0, one launch (start us, length us, event | category | flops | bytes accessed | tf_op | source)
XLA Modules:
  0.0 167.4 jit_solution(3971053970301196801)
XLA Ops:
  0.0 1.1 slice.71.src
  1.1 1.0 slice.72
  2.1 0.7 convert_bitcast_fusion.1
  2.7 0.7 convert_element_type.90
  3.4 0.7 convert_element_type.91
  4.5 37.3 %gather0.1 = bf16[1024,1408]{1,0:T(8,128)(2,1)S(1)} custom-call(bf16[128,1408]{1,0:T(8,128)(2,1)S(1)} %concatenate.23.src), custom_call_target="tpu_custom_call" | custom-call | bytes 62914560 | tf_op jit(solution)/shard_map/gather0/pallas_call | solution.py:226
  41.8 1.6 copy-done.1
  44.1 0.2 fusion.24
  44.6 3.5 %convolution_convert_fusion.1 = bf16[2,256,1280]{2,1,0:T(8,128)(2,1)S(1)} fusion(bf16[1024,1408]{1,0:T(8,128)(2,1)} %copy-done.1, s32[2,1024]{1,0:T(2,128)S(1)} %bitcast.64), kind=kOutput, calls=%fused_computation.4 | convolution fusion | flops 1343356928 | bytes 3940352 | tf_op jit(solution)/shard_map/rst,td->rsd/dot_general | solution.py:346
  48.2 1.6 collective-permute-start
  49.7 21.3 %gather2.1 = bf16[1024,768]{1,0:T(8,128)(2,1)S(1)} custom-call(bf16[128,768]{1,0:T(8,128)(2,1)S(1)} %slice.71.src), custom_call_target="tpu_custom_call" | custom-call | bytes 62914560 | tf_op jit(solution)/shard_map/gather2/pallas_call | solution.py:226
  71.0 1.3 fusion.8
  72.4 0.5 collective-permute-start.2
  73.1 7.4 %collective-permute-done.2 = bf16[256,768]{1,0:T(8,128)(2,1)S(1)} collective-permute-done((bf16[256,768]{1,0:T(8,128)(2,1)S(1)}, bf16[256,768]{1,0:T(8,128)(2,1)S(1)}, u32[]{:S(2)}, u32[]{:S(2)}) %collective-permute-start.2) | collective-permute-done | bytes 393248 | tf_op jit(solution)/shard_map/ppermute | solution.py:273
  80.7 2.3 %collective-permute-done.3 = bf16[512,768]{1,0:T(8,128)(2,1)S(1)} collective-permute-done((bf16[512,768]{1,0:T(8,128)(2,1)S(1)}, bf16[512,768]{1,0:T(8,128)(2,1)S(1)}, u32[]{:S(2)}, u32[]{:S(2)}) %collective-permute-start.3) | collective-permute-done | bytes 786464 | tf_op jit(solution)/shard_map/ppermute | solution.py:268
  83.0 2.3 %fusion.5 = f32[1024,384]{1,0:T(8,128)S(1)} fusion(bf16[1,2048,384]{2,1,0:T(8,128)(2,1)S(1)} %copy-done, bf16[512,768]{1,0:T(8,128)(2,1)S(1)} %collective-permute-done.3, bf16[256,768]{1,0:T(8,128)(2,1)S(1)} %collective-permute-done.2, bf16[256,768]{1,0:T(8,128)(2,1)S(1)} %get-tuple-element.28, bf16[512,1280]{1,0:T(8,128)(2,1)S(1)} %collective-permute-done.1, ...), kind=kOutput, calls=%fused_computation.14 | convolution fusion | flops 1635778560 | bytes 7340032 | tf_op jit(solution)/shard_map/dot_general | solution.py:351
  85.3 2.4 %multiply_convert_fusion = bf16[1024,384]{1,0:T(8,128)(2,1)S(1)} fusion(f32[1024,384]{1,0:T(8,128)S(1)} %fusion.5, bf16[1,2048,384]{2,1,0:T(8,128)(2,1)S(1)} %copy-done.2, bf16[512,768]{1,0:T(8,128)(2,1)S(1)} %collective-permute-done.3, bf16[256,768]{1,0:T(8,128)(2,1)S(1)} %collective-permute-done.2, bf16[256,768]{1,0:T(8,128)(2,1)S(1)} %get-tuple-element.28, ...), kind=kOutput, calls=%fused_computation.18 | convolution fusion | flops 1638137856 | bytes 8126464 | tf_op jit(solution)/shard_map/dot_general | solution.py:352
  87.8 1.0 convolution_convert_fusion.2
  89.0 2.2 %collective-permute-done.4 = bf16[512,768]{1,0:T(8,128)(2,1)S(1)} collective-permute-done((bf16[512,768]{1,0:T(8,128)(2,1)S(1)}, bf16[512,768]{1,0:T(8,128)(2,1)S(1)}, u32[]{:S(2)}, u32[]{:S(2)}) %collective-permute-start.4) | collective-permute-done | bytes 786464 | tf_op jit(solution)/shard_map/ppermute | solution.py:268
  91.1 0.2 add_convert_fusion.1
  91.4 1.5 convolution_convert_fusion
  93.0 0.2 collective-permute-start.5
  93.2 0.3 collective-permute-start.7
  93.6 2.5 %collective-permute-done.5 = bf16[512,1280]{1,0:T(8,128)(2,1)S(1)} collective-permute-done((bf16[512,1280]{1,0:T(8,128)(2,1)S(1)}, bf16[512,1280]{1,0:T(8,128)(2,1)S(1)}, u32[]{:S(2)}, u32[]{:S(2)}) %collective-permute-start.5) | collective-permute-done | bytes 1310752 | tf_op jit(solution)/shard_map/ppermute | solution.py:268
  96.1 0.3 add_convert_fusion
  96.5 0.3 collective-permute-start.6
  96.8 8.4 %collective-permute-done.7 = bf16[256,768]{1,0:T(8,128)(2,1)S(1)} collective-permute-done((bf16[256,768]{1,0:T(8,128)(2,1)S(1)}, bf16[256,768]{1,0:T(8,128)(2,1)S(1)}, u32[]{:S(2)}, u32[]{:S(2)}) %collective-permute-start.7) | collective-permute-done | bytes 393248 | tf_op jit(solution)/shard_map/ppermute | solution.py:273
  105.3 1.7 %bitcast_convert_fusion.1.part = bf16[1024,768]{1,0:T(8,128)(2,1)S(1)} fusion(bf16[2,1024]{1,0:T(2,128)(2,1)S(1)} %bitcast.68, s32[2,1024]{1,0:T(2,128)S(1)} %bitcast.66, bf16[1,256,768]{2,1,0:T(8,128)(2,1)S(1)} %bitcast.72, bf16[1,256,768]{2,1,0:T(8,128)(2,1)S(1)} %get-tuple-element.26), kind=kOutput, calls=%fused_computation.3 | convolution fusion | flops 807534592 | bytes 2371584 | tf_op jit(solution)/shard_map/rst,rsd->td/dot_general | solution.py:370
  107.0 25.8 %scatter1.1 = bf16[128,768]{1,0:T(8,128)(2,1)S(1)} custom-call(bf16[1024,768]{1,0:T(8,128)(2,1)S(1)} %bitcast_convert_fusion.1.part), custom_call_target="tpu_custom_call" | custom-call | bytes 62914560 | tf_op jit(solution)/shard_map/scatter1/pallas_call | solution.py:248
  133.0 2.1 %bitcast_convert_fusion.part = bf16[1024,1280]{1,0:T(8,128)(2,1)S(1)} fusion(bf16[2,256,1280]{2,1,0:T(8,128)(2,1)S(1)} %pad_maximum_fusion.1, bf16[2,1024]{1,0:T(2,128)(2,1)S(1)} %bitcast.69, s32[2,1024]{1,0:T(2,128)S(1)} %bitcast.67), kind=kOutput, calls=%fused_computation | convolution fusion | flops 1344536576 | bytes 3944448 | tf_op jit(solution)/shard_map/rst,rsd->td/dot_general | solution.py:370
  135.0 31.4 %scatter3.1 = bf16[128,1280]{1,0:T(8,128)(2,1)S(1)} custom-call(bf16[1024,1280]{1,0:T(8,128)(2,1)S(1)} %bitcast_convert_fusion.part), custom_call_target="tpu_custom_call" | custom-call | bytes 62914560 | tf_op jit(solution)/shard_map/scatter3/pallas_call | solution.py:248
  166.5 0.8 pad_maximum_fusion.3
  (41 shorter events, 2.4 us)
Async XLA Ops:
  0.0 83.0 %copy-start = (bf16[1,2048,384]{2,1,0:T(8,128)(2,1)S(1)}, bf16[1,2048,384]{2,1,0:T(8,128)(2,1)}, u32[]{:S(2)}) copy-start(bf16[1,2048,384]{2,1,0:T(8,128)(2,1)} %param.11) | copy-start | bytes 4718596
  41.8 1.6 copy-start.1
  48.2 24.8 %collective-permute-start = (bf16[256,1280]{1,0:T(8,128)(2,1)S(1)}, bf16[256,1280]{1,0:T(8,128)(2,1)S(1)}, u32[]{:S(2)}, u32[]{:S(2)}) collective-permute-start(bf16[256,1280]{1,0:T(8,128)(2,1)S(1)} %get-tuple-element.25), channel_id=1, source_target_pairs={{0,2},{1,3},{2,0},{3,1},{4,6},{5,7},{6,4},{7,5},{8,10},{9,11},{10,... | collective-permute-start | bytes 1966088 | tf_op jit(solution)/shard_map/ppermute | solution.py:273
  72.4 8.1 %collective-permute-start.2 = (bf16[256,768]{1,0:T(8,128)(2,1)S(1)}, bf16[256,768]{1,0:T(8,128)(2,1)S(1)}, u32[]{:S(2)}, u32[]{:S(2)}) collective-permute-start(bf16[256,768]{1,0:T(8,128)(2,1)S(1)} %get-tuple-element.29), channel_id=1, source_target_pairs={{0,2},{1,3},{2,0},{3,1},{4,6},{5,7},{6,4},{7,5},{8,10},{9,11},{10,... | collective-permute-start | bytes 1179656 | tf_op jit(solution)/shard_map/ppermute | solution.py:273
  73.1 9.9 %collective-permute-start.1 = (bf16[512,1280]{1,0:T(8,128)(2,1)S(1)}, bf16[512,1280]{1,0:T(8,128)(2,1)S(1)}, u32[]{:S(2)}, u32[]{:S(2)}) collective-permute-start(bf16[512,1280]{1,0:T(8,128)(2,1)S(1)} %pad_maximum_fusion), channel_id=1, source_target_pairs={{0,1},{1,0},{2,3},{3,2},{4,5},{5,4},{6,7},{7,6},{8,9},{9,8},{10,11... | collective-permute-start | bytes 3932168 | tf_op jit(solution)/shard_map/ppermute | solution.py:268
  80.6 4.7 %copy-start.2 = (bf16[1,2048,384]{2,1,0:T(8,128)(2,1)S(1)}, bf16[1,2048,384]{2,1,0:T(8,128)(2,1)}, u32[]{:S(2)}) copy-start(bf16[1,2048,384]{2,1,0:T(8,128)(2,1)} %param.12) | copy-start | bytes 4718596
  80.6 2.4 %collective-permute-start.3 = (bf16[512,768]{1,0:T(8,128)(2,1)S(1)}, bf16[512,768]{1,0:T(8,128)(2,1)S(1)}, u32[]{:S(2)}, u32[]{:S(2)}) collective-permute-start(bf16[512,768]{1,0:T(8,128)(2,1)S(1)} %pad_maximum_fusion.2), channel_id=1, source_target_pairs={{0,1},{1,0},{2,3},{3,2},{4,5},{5,4},{6,7},{7,6},{8,9},{9,8},{10,11... | collective-permute-start | bytes 2359304 | tf_op jit(solution)/shard_map/ppermute | solution.py:268
  85.3 2.4 %copy-start.3 = (bf16[1,384,2048]{2,1,0:T(8,128)(2,1)S(1)}, bf16[1,384,2048]{2,1,0:T(8,128)(2,1)}, u32[]{:S(2)}) copy-start(bf16[1,384,2048]{2,1,0:T(8,128)(2,1)} %param.13) | copy-start | bytes 4718596
  88.8 2.4 %collective-permute-start.4 = (bf16[512,768]{1,0:T(8,128)(2,1)S(1)}, bf16[512,768]{1,0:T(8,128)(2,1)S(1)}, u32[]{:S(2)}, u32[]{:S(2)}) collective-permute-start(bf16[512,768]{1,0:T(8,128)(2,1)S(1)} %slice.103), channel_id=1, source_target_pairs={{0,1},{1,0},{2,3},{3,2},{4,5},{5,4},{6,7},{7,6},{8,9},{9,8},{10,11... | collective-permute-start | bytes 2359304 | tf_op jit(solution)/shard_map/ppermute | solution.py:268
  93.0 3.1 %collective-permute-start.5 = (bf16[512,1280]{1,0:T(8,128)(2,1)S(1)}, bf16[512,1280]{1,0:T(8,128)(2,1)S(1)}, u32[]{:S(2)}, u32[]{:S(2)}) collective-permute-start(bf16[512,1280]{1,0:T(8,128)(2,1)S(1)} %slice.106), channel_id=1, source_target_pairs={{0,1},{1,0},{2,3},{3,2},{4,5},{5,4},{6,7},{7,6},{8,9},{9,8},{10,11... | collective-permute-start | bytes 3932168 | tf_op jit(solution)/shard_map/ppermute | solution.py:268
  93.2 12.1 %collective-permute-start.7 = (bf16[256,768]{1,0:T(8,128)(2,1)S(1)}, bf16[256,768]{1,0:T(8,128)(2,1)S(1)}, u32[]{:S(2)}, u32[]{:S(2)}) collective-permute-start(bf16[256,768]{1,0:T(8,128)(2,1)S(1)} %get-tuple-element.27), channel_id=1, source_target_pairs={{0,2},{1,3},{2,0},{3,1},{4,6},{5,7},{6,4},{7,5},{8,10},{9,11},{10,... | collective-permute-start | bytes 1179656 | tf_op jit(solution)/shard_map/ppermute | solution.py:273
  96.5 36.4 %collective-permute-start.6 = (bf16[256,1280]{1,0:T(8,128)(2,1)S(1)}, bf16[256,1280]{1,0:T(8,128)(2,1)S(1)}, u32[]{:S(2)}, u32[]{:S(2)}) collective-permute-start(bf16[256,1280]{1,0:T(8,128)(2,1)S(1)} %get-tuple-element.23), channel_id=1, source_target_pairs={{0,2},{1,3},{2,0},{3,1},{4,6},{5,7},{6,4},{7,5},{8,10},{9,11},{10,... | collective-permute-start | bytes 1966088 | tf_op jit(solution)/shard_map/ppermute | solution.py:273
where the time goes:
time: 168 us; the launch traced here: 167 us
  Pallas kernels  116 us (69%)
  waiting for transfers between devices  22.8 us (14%)
  matrix products  15.9 us (9%)
  local copies, waits for them, and re-layouts  5.07 us (3%)
  other arithmetic  4.17 us (2%)
  starting transfers between devices  3.37 us (2%)
    pallas_call x2, Pallas kernels, gather_dp(): pl.pallas_call(functools.partial(gather_kernel, ring), name='gather%d' %...  58.5 us
    pallas_call x2, Pallas kernels, scatter_dp(): pl.pallas_call(functools.partial(scatter_kernel, ring), name='scatter%d'...  57.3 us
    ppermute x4, waiting for transfers between devices, turn(): return lax.ppermute(block, 'expert', route)  15.8 us
    ppermute x4, waiting for transfers between devices, swap_cores(): return lax.ppermute(block, 'expert', [(c, c ^ 1) for c in range(col_size)])  6.92 us
    dot_general x2, matrix products, on_device(): jnp.einsum('rst,td->rsd', spots, columns[n], preferred_element_type=F32)  4.79 us
    dot_general x2, matrix products, on_device(): jnp.einsum('rst,rsd->td', weights, home, preferred_element_type=F32)  3.75 us
  transfers between devices with their start and end apart: 8, of which 5 were waited for; matrix products, arithmetic and copies ran while one was open for 2% of the time, Pallas kernels for 28%

commit v1 on v0

v1 whole, which is shorter than its diff:
```python
import functools

import jax
import jax.numpy as jnp
from jax import lax
from jax.experimental import pallas as pl
from jax.experimental.pallas import tpu as pltpu
from jax.sharding import PartitionSpec as P

BF = jnp.bfloat16
F32 = jnp.float32
FAR = 4096.0
FORTH = (4, 2, 2)
BACK = (2, 4, 2)
MESH = pl.DeviceIdType.MESH


def cuts(width, shares):
    unit = width // sum(shares)
    spans, begin = [], 0
    for share in shares:
        spans.append((begin, unit * share))
        begin += unit * share
    return spans


class Wires:
    def __init__(self):
        self.sent = []

    def copy(self, src, dst, ssem, rsem, to):
        return pltpu.make_async_remote_copy(
            src_ref=src, dst_ref=dst, send_sem=ssem, recv_sem=rsem,
            device_id=to, device_id_type=MESH,
        )

    def send(self, src, dst, ssem, rsem, to, cond=None):
        def go():
            self.copy(src, dst, ssem, rsem, to).start()

        if cond is None:
            go()
        else:
            pl.when(cond)(go)
        self.sent.append((src, dst, ssem, rsem, to, cond))

    def arrive(self, dst, rsem, to):
        self.copy(dst, dst, rsem, rsem, to).wait_recv()

    def finish(self):
        sent, self.sent = self.sent, []
        for *args, cond in sent:
            moved = self.copy(*args)
            if cond is None:
                moved.wait_send()
            else:
                pl.when(cond)(moved.wait_send)


def layer_kernel(shape, tokens, ids, probs, limits, gate, up, down, out, *scratch):
    dp, rows_y, cap, share = shape
    line = dp // 2
    plane = 2 * rows_y
    count, width = tokens.shape
    half = width // 2
    ff = gate.shape[1]
    forth, back = cuts(half, FORTH), cuts(half, FORTH if share else BACK)
    nf, nb = len(forth), len(back)

    scratch = list(scratch)

    def take(n):
        got = scratch[:n]
        del scratch[:n]
        return got

    w1, w2, own_meta, meta, acc, hidden = take(6)
    tok, picked, rows_in = take(nf), take(nf), take(nf)
    sent_out, slots_in, ring_in = take(nb), take(nb), take(nb)
    part = tok if share else take(nb)
    (choose,) = take(1)
    blend = choose if share else take(1)[0]
    (m_s, m_r, w_s, w_r, w_l, x_s, up_s, dn_s, tok_r, p_s, p_r) = take(11)
    (q_s, q_r, ru_s, ru_r, rd_s, rd_r, f_s, f_r) = take(8)

    d, c = lax.axis_index("dp"), lax.axis_index("expert")
    z, x = lax.div(d, 2), lax.rem(d, 2)
    y, k = lax.div(c, 2), lax.rem(c, 2)
    here = x * rows_y + y
    across = {"dp": z * 2 + 1 - x, "expert": c}
    ahead = {"dp": lax.rem(d + 2, dp), "expert": c}
    behind = {"dp": lax.rem(d + dp - 2, dp), "expert": c}
    twin = {"dp": d, "expert": c + 1 - 2 * k}
    has_up, has_dn = z < line - 1, z > 0
    wires = Wires()

    def column_peer(s):
        return {"dp": lax.rem(d + s, dp), "expert": c}

    def plane_peer(dx, dy):
        to_x, to_y = lax.rem(x + dx, 2), lax.rem(y + dy, rows_y)
        return to_x, to_y, {"dp": z * 2 + to_x, "expert": to_y * 2 + k}

    offsets = [(dx, dy) for dy in range(rows_y) for dx in range(2) if dx or dy][::-1]

    barrier = pltpu.get_barrier_semaphore()
    peers = [column_peer(s) for s in range(1, dp)] + [twin]
    peers += [plane_peer(dx, dy)[2] for dx, dy in offsets if dy]
    for peer in peers:
        pl.semaphore_signal(barrier, inc=1, device_id=peer, device_id_type=MESH)

    local = [
        pltpu.make_async_copy(gate, w1.at[:, pl.ds(0, ff)], w_l.at[0]),
        pltpu.make_async_copy(up, w1.at[:, pl.ds(2 * ff, ff)], w_l.at[1]),
        pltpu.make_async_copy(down, w2.at[pl.ds(0, ff)], w_l.at[2]),
    ]
    for copy in local:
        copy.start()

    lane = lax.broadcasted_iota(jnp.int32, (count, count), 1)
    deep = lax.broadcasted_iota(jnp.int32, (count, count), 0)
    chosen = jnp.zeros((count, count), F32)
    weight = jnp.zeros((count, count), F32)
    for j in range(ids.shape[1]):
        match = lane == ids[:, j : j + 1]
        chosen = chosen + jnp.where(match, 1.0, 0.0)
        weight = weight + jnp.where(match, probs[:, j : j + 1], 0.0)
    lower = jnp.where(lane < deep, 1.0, 0.0).astype(BF)
    rank = jnp.dot(lower, chosen.astype(BF), preferred_element_type=F32)
    experts = limits.shape[1]
    limit = jnp.concatenate(
        [limits[...].astype(F32), jnp.zeros((1, count - experts), F32)], axis=1
    ) if experts < count else limits[...].astype(F32)
    rank = jnp.where((chosen > 0) & (rank < limit), rank, FAR)
    rank, weight = rank.T, weight.T
    for zz in range(line):
        own_meta[zz, :plane] = rank[zz * plane : (zz + 1) * plane]
        own_meta[zz, plane:] = weight[zz * plane : (zz + 1) * plane]
    meta[d] = own_meta[z]
    for j, (begin, w) in enumerate(forth):
        mine = pl.ds(pl.multiple_of(x * half + begin, 128), w)
        tok[j][pl.ds(pl.multiple_of(d * count, count), count)] = tokens[:, mine]

    pl.semaphore_wait(barrier, len(peers))

    def block(o):
        return pl.ds(pl.multiple_of(o * count, count), count)

    for s in range(1, dp):
        to = column_peer(s)
        wires.send(own_meta.at[lax.div(to["dp"], 2)], meta.at[d], m_s.at[s], m_r.at[d], to)

    def send_own(j):
        begin, w = forth[j]
        src = tokens.at[:, pl.ds(pl.multiple_of(x * half + begin, 128), w)]
        dst = tok[j].at[block(d)]
        wires.send(src, dst, up_s.at[j, d], tok_r.at[j, d], ahead, has_up)
        wires.send(src, dst, dn_s.at[j, d], tok_r.at[j, d], behind, has_dn)

    def send_cross(j):
        begin, w = forth[j]
        src = tokens.at[:, pl.ds(pl.multiple_of((1 - x) * half + begin, 128), w)]
        wires.send(src, tok[j].at[block(d)], x_s.at[j], tok_r.at[j, d], across)

    def collect(j):
        def ref(o):
            return tok[j].at[block(o)]

        o = z * 2 + 1 - x
        wires.arrive(ref(o), tok_r.at[j, o], across)
        wires.send(ref(o), ref(o), up_s.at[j, o], tok_r.at[j, o], ahead, has_up)
        wires.send(ref(o), ref(o), dn_s.at[j, o], tok_r.at[j, o], behind, has_dn)
        if j + 1 < nf:
            send_own(j + 1)
        for s in range(1, line):
            for xx in (x, 1 - x):
                low, high = z - s >= 0, z + s < line
                o = lax.max(z - s, 0) * 2 + xx

                @pl.when(low)
                def _():
                    wires.arrive(ref(o), tok_r.at[j, o], across)

                wires.send(
                    ref(o), ref(o), up_s.at[j, o], tok_r.at[j, o], ahead, low & has_up
                )
                o2 = lax.min(z + s, line - 1) * 2 + xx

                @pl.when(high)
                def _():
                    wires.arrive(ref(o2), tok_r.at[j, o2], across)

                wires.send(
                    ref(o2), ref(o2), dn_s.at[j, o2], tok_r.at[j, o2], behind, high & has_dn
                )

    send_own(0)
    for j in range(nf):
        send_cross(j)
    wires.send(gate, w1.at[:, pl.ds(ff, ff)], w_s.at[0], w_r.at[0], twin)
    wires.send(up, w1.at[:, pl.ds(3 * ff, ff)], w_s.at[1], w_r.at[1], twin)
    wires.send(down, w2.at[pl.ds(ff, ff)], w_s.at[2], w_r.at[2], twin)

    def wait_weights():
        for copy in local:
            copy.wait()
        wires.arrive(w1.at[:, pl.ds(ff, ff)], w_r.at[0], twin)
        wires.arrive(w1.at[:, pl.ds(3 * ff, ff)], w_r.at[1], twin)
        wires.arrive(w2.at[pl.ds(ff, ff)], w_r.at[2], twin)

    is_rank = lax.broadcasted_iota(jnp.int32, (2 * plane, count), 0) < plane

    def number_slots():
        for s in range(1, dp):
            o = lax.rem(d + s, dp)
            wires.arrive(meta.at[o], m_r.at[o], across)
        offset = jnp.zeros((2 * plane, 1), F32)
        for o in range(dp):
            given = meta[o]
            valid = is_rank & (given < FAR)
            slot = given + offset
            offset = offset + jnp.sum(jnp.where(valid, 1.0, 0.0), axis=1, keepdims=True)
            slot = jnp.where(valid & (slot < float(cap)), slot, FAR)
            meta[o] = jnp.where(is_rank, slot, given)

    spot = lax.broadcasted_iota(jnp.int32, (cap, count), 0).astype(F32)

    def build_choose():
        for p in range(plane):
            for o in range(dp):
                hit = spot == meta[o, p : p + 1]
                choose[p * cap : (p + 1) * cap, o * count : (o + 1) * count] = jnp.where(
                    hit, 1.0, 0.0
                ).astype(BF)

    spot_t = lax.broadcasted_iota(jnp.int32, (count, cap), 1).astype(F32)

    def weigh_choose():
        for p in range(plane):
            for o in range(dp):
                hit = spot == meta[o, p : p + 1]
                piece = jnp.where(hit, meta[o, plane + p : plane + p + 1], 0.0).astype(BF)
                choose[p * cap : (p + 1) * cap, o * count : (o + 1) * count] = piece

    def build_blend():
        deep_rows = 2 * plane
        group = count // deep_rows
        for g in range(0, dp, group):
            n = min(group, dp - g)
            value = meta[g : g + n].reshape(n * deep_rows, count)
            if n < group:
                value = jnp.concatenate(
                    [value, jnp.zeros((count - n * deep_rows, count), F32)], axis=0
                )
            value = value.T
            for i in range(n):
                o = g + i
                for p in range(plane):
                    a = i * deep_rows + p
                    hit = spot_t == value[:, a : a + 1]
                    b = a + plane
                    piece = jnp.where(hit, value[:, b : b + 1], 0.0).astype(BF)
                    blend[o * count : (o + 1) * count, p * cap : (p + 1) * cap] = piece

    def pick(j):
        begin, w = forth[j]
        for dx, dy in offsets + [(0, 0)]:
            to_x, to_y, to = plane_peer(dx, dy)
            there = to_x * rows_y + to_y
            got = jnp.dot(
                choose[pl.ds(pl.multiple_of(there * cap, cap), cap)],
                tok[j][...],
                preferred_element_type=F32,
            ).astype(BF)
            mine = pl.ds(pl.multiple_of(y * cap, cap), cap)
            if dx or dy:
                n = dx * rows_y + dy
                picked[j][n] = got
                wires.send(
                    picked[j].at[n], rows_in[j].at[x, mine], p_s.at[j, n], p_r.at[j, n], to
                )
            else:
                rows_in[j][x, mine] = got

    def expand(j):
        begin, w = forth[j]
        for dx, dy in offsets:
            n = dx * rows_y + dy
            from_x = lax.rem(x + dx, 2)
            from_y = lax.rem(y + rows_y - dy, rows_y)
            spot_in = rows_in[j].at[from_x, pl.ds(pl.multiple_of(from_y * cap, cap), cap)]
            wires.arrive(spot_in, p_r.at[j, n], across)
        for n in range(0, 4 * ff, 2 * ff):
            cols = pl.ds(n, 2 * ff)
            value = jnp.dot(rows_in[j][0], w1[begin : begin + w, cols], preferred_element_type=F32)
            value = value + jnp.dot(
                rows_in[j][1], w1[half + begin : half + begin + w, cols],
                preferred_element_type=F32,
            )
            if j == 0:
                acc[:, cols] = value
            else:
                acc[:, cols] += value

    number_slots()
    build_choose()
    for j in range(nf):
        collect(j)
        if j == 0 and not share:
            build_blend()
        pick(j)
        if j == 1:
            wait_weights()
        if j > 0:
            expand(j - 1)
    if nf == 1:
        wait_weights()
    expand(nf - 1)

    gated = acc[:, : 2 * ff]
    hidden[...] = (gated / (1.0 + jnp.exp(-gated)) * acc[:, 2 * ff :]).astype(BF)
    if share:
        wires.finish()
        weigh_choose()

    def project(j):
        begin, w = back[j]
        for dx, dy in offsets + [(0, 0)]:
            to_x, to_y, to = plane_peer(dx, dy)
            cols = pl.ds(pl.multiple_of(to_x * half + begin, 128), w)
            value = jnp.dot(
                hidden[pl.ds(pl.multiple_of(to_y * cap, cap), cap)],
                w2[:, cols],
                preferred_element_type=F32,
            ).astype(BF)
            home = pl.ds(pl.multiple_of(here * cap, cap), cap)
            if dx or dy:
                n = dx * rows_y + dy
                sent_out[j][n] = value
                wires.send(
                    sent_out[j].at[n], slots_in[j].at[home], q_s.at[j, n], q_r.at[j, n], to
                )
            else:
                slots_in[j][home] = value

    def mix(j):
        for dx, dy in offsets:
            n = dx * rows_y + dy
            from_x = lax.rem(x + dx, 2)
            from_y = lax.rem(y + rows_y - dy, rows_y)
            home = pl.ds(pl.multiple_of((from_x * rows_y + from_y) * cap, cap), cap)
            wires.arrive(slots_in[j].at[home], q_r.at[j, n], across)
        value = slots_in[j][...]
        if share:
            got = lax.dot_general(
                blend[...], value, (((0,), (0,)), ((), ())), preferred_element_type=F32
            )
        else:
            got = jnp.dot(blend[...], value, preferred_element_type=F32)
        part[j][...] = got.astype(BF)

    def pair(o):
        return pl.ds(o * 2 * count, 2 * count)

    def hop(j, o, upward, cond):
        rows = part[j].at[pair(o)]
        slot = ring_in[j].at[o + 1 if upward else o]
        ssem, rsem = (ru_s, ru_r) if upward else (rd_s, rd_r)
        wires.send(
            rows, slot, ssem.at[j, o], rsem.at[j, o], ahead if upward else behind, cond
        )

    def join(j, o, upward, cond):
        rsem = ru_r if upward else rd_r
        slot = ring_in[j].at[o + 1 if upward else o]

        @pl.when(cond)
        def _():
            wires.arrive(slot, rsem.at[j, o], across)
            part[j][pair(o)] = (part[j][pair(o)].astype(F32) + slot[...].astype(F32)).astype(BF)

    def reduce_ends(j):
        for t in range(line - 1):
            hop(j, line - 1 - t, True, z == 0)
            hop(j, t, False, z == line - 1)

    def reduce_rest(j):
        for t in range(line - 1):
            o = line - 1 - t
            cond = (z > 0) & (z < o)
            join(j, o, True, cond)
            hop(j, o, True, cond)
            cond = (z < line - 1) & (z > t)
            join(j, t, False, cond)
            hop(j, t, False, cond)

    def settle(j):
        begin, w = back[j]
        rows = pl.ds(pl.multiple_of(z * 2 * count, 2 * count), 2 * count)

        @pl.when(has_dn)
        def _():
            slot = ring_in[j].at[z + 1]
            wires.arrive(slot, ru_r.at[j, z], across)
            part[j][rows] = (part[j][rows].astype(F32) + slot[...].astype(F32)).astype(BF)

        @pl.when(has_up)
        def _():
            slot = ring_in[j].at[z]
            wires.arrive(slot, rd_r.at[j, z], across)
            part[j][rows] = (part[j][rows].astype(F32) + slot[...].astype(F32)).astype(BF)

        cols = pl.ds(pl.multiple_of(x * half + begin, 128), w)
        wires.send(
            part[j].at[block(z * 2 + 1 - x)], out.at[:, cols], f_s.at[j], f_r.at[j], across
        )
        out[:, cols] = part[j][block(d)]

    project(0)
    for j in range(nb):
        if j + 1 < nb:
            project(j + 1)
        mix(j)
        reduce_ends(j)
        if j > 0:
            reduce_rest(j - 1)
            settle(j - 1)
    reduce_rest(nb - 1)
    settle(nb - 1)
    for j, (begin, w) in enumerate(back):
        cols = pl.ds(pl.multiple_of((1 - x) * half + begin, 128), w)
        wires.arrive(out.at[:, cols], f_r.at[j], across)
    wires.finish()


def on_device(tokens, expert_ids, route_probs, shard_limit, gate_proj, up_proj, down_proj):
    count, width = tokens.shape
    top = expert_ids.shape[1]
    experts = shard_limit.shape[1]
    dp, cols = lax.axis_size("dp"), lax.axis_size("expert")
    rows_y = cols // 2
    cap = dp * (count * top // experts) // 2
    line, plane, half = dp // 2, 2 * rows_y, width // 2
    ff = gate_proj.shape[2]
    all_tok, all_slots, rows = dp * count, plane * cap, rows_y * cap
    share = all_tok * all_slots > 1 << 21
    forth, back = cuts(half, FORTH), cuts(half, FORTH if share else BACK)
    nf, nb = len(forth), len(back)
    scratch = [
        pltpu.VMEM((width, 4 * ff), BF),
        pltpu.VMEM((2 * ff, width), BF),
        pltpu.VMEM((line, 2 * plane, count), F32),
        pltpu.VMEM((dp, 2 * plane, count), F32),
        pltpu.VMEM((rows, 4 * ff), F32),
        pltpu.VMEM((rows, 2 * ff), BF),
    ]
    scratch += [pltpu.VMEM((all_tok, w), BF) for _, w in forth]
    scratch += [pltpu.VMEM((plane, cap, w), BF) for _, w in forth]
    scratch += [pltpu.VMEM((2, rows, w), BF) for _, w in forth]
    scratch += [pltpu.VMEM((plane, cap, w), BF) for _, w in back]
    scratch += [pltpu.VMEM((all_slots, w), BF) for _, w in back]
    scratch += [pltpu.VMEM((line + 1, 2 * count, w), BF) for _, w in back]
    if not share:
        scratch += [pltpu.VMEM((all_tok, w), BF) for _, w in back]
    scratch += [pltpu.VMEM((all_slots, all_tok), BF)]
    if not share:
        scratch += [pltpu.VMEM((all_tok, all_slots), BF)]
    DMA = pltpu.SemaphoreType.DMA
    scratch += [DMA((dp,)), DMA((dp,)), DMA((3,)), DMA((3,)), DMA((3,)), DMA((nf,))]
    scratch += [DMA((nf, dp)), DMA((nf, dp)), DMA((nf, dp)), DMA((nf, plane)), DMA((nf, plane))]
    scratch += [DMA((nb, plane)), DMA((nb, plane))] + [DMA((nb, line))] * 4
    scratch += [DMA((nb,)), DMA((nb,))]
    vm, anywhere = pl.BlockSpec(memory_space=pltpu.VMEM), pl.BlockSpec(memory_space=pl.ANY)
    return pl.pallas_call(
        functools.partial(layer_kernel, (dp, rows_y, cap, share)),
        name="layer",
        out_shape=jax.ShapeDtypeStruct((count, width), BF),
        in_specs=[vm] * 4 + [anywhere] * 3,
        out_specs=vm,
        scratch_shapes=scratch,
        compiler_params=pltpu.CompilerParams(
            collective_id=0, has_side_effects=True, vmem_limit_bytes=62 << 20
        ),
    )(tokens, expert_ids, route_probs, shard_limit, gate_proj[0], up_proj[0], down_proj[0])


def solution(mesh):
    rows = P(("dp", "expert"), None)
    blocks = P(("dp", "expert"), None, None)
    return jax.shard_map(
        on_device,
        mesh=mesh,
        in_specs=(rows, rows, rows, rows, blocks, blocks, blocks),
        out_specs=rows,
        check_vma=False,
    )
```

time: 168 us -> 130 us (0.77)
  waiting for transfers between devices: 22.8 us -> 0 us
  matrix products: 15.9 us -> 0 us
  Pallas kernels: 116 us -> 125 us
  other arithmetic: 4.17 us -> 0 us
  starting transfers between devices: 3.37 us -> 0 us
    ppermute x8 -> x0, waiting for transfers between devices: 22.8 us -> none  [the longest x4 15.8 us: turn(): return lax.ppermute(block, 'expert', route)]
    dot_general x9 -> x0, matrix products: 15.9 us -> none  [the longest x2 4.79 us: on_device(): jnp.einsum('rst,td->rsd', spots, columns[n], preferred_element_type=F32)]
    pallas_call x4 -> x1, Pallas kernels: 116 us -> 125 us  [on_device(): pl.pallas_call(functools.partial(layer_kernel, (dp, rows_y, cap, share)),...]
    ppermute x8 -> x0, starting transfers between devices: 3.37 us -> none  [the longest x4 2.82 us: turn(): return lax.ppermute(block, 'expert', route)]
    unnamed x10 -> x3, local copies, waits for them, and re-layouts: 1.64 us -> 4.7 us
    slice x11 -> x0, local copies, waits for them, and re-layouts: 2.9 us -> none  [the longest x1 1.06 us: on_device(): tokens[:, low:high]]
    convert_element_type x7 -> x0, other arithmetic: 2 us -> none  [the longest x1 0.69 us: on_device(): expert_ids.astype(BF)]
  transfers between devices with their start and end apart: 8 -> 0, of which waited for: 5 -> 0; matrix products, arithmetic and copies ran while one was open for 2% -> 0% of each run, Pallas kernels for 28% -> 0%
where the time goes in v1:
time: 130 us
  Pallas kernels  125 us (96%)
  local copies, waits for them, and re-layouts  4.7 us (4%)
    pallas_call x1, Pallas kernels, on_device(): pl.pallas_call(functools.partial(layer_kernel, (dp, rows_y, cap, share)),...  125 us
    unnamed x3, local copies, waits for them, and re-layouts  4.7 us

profile of v1, /device:TPU:0, one launch (start us, length us, event | category | flops | bytes accessed | tf_op | source)
XLA Modules:
  0.0 129.7 jit_solution(13129720841409444289)
XLA Ops:
  0.0 1.4 %copy.8.ids = s32[128,8]{1,0:T(8,128)} copy(s32[128,8]{0,1:T(8,128)} %param.8) | data formatting | bytes 8192 | tf_op args[1]
  1.4 1.4 %copy.9.probs = f32[128,8]{1,0:T(8,128)} copy(f32[128,8]{0,1:T(8,128)} %param.9) | data formatting | bytes 8192 | tf_op args[2]
  2.8 125.0 %layer.1 = bf16[128,2048]{1,0:T(8,128)(2,1)} custom-call(bf16[128,2048]{1,0:T(8,128)(2,1)} %tokens.1, s32[128,8]{1,0:T(8,128)} %copy.8.ids, f32[128,8]{1,0:T(8,128)} %copy.9.probs, s32[1,16]{1,0:T(1,128)} %limits.1, bf16[2048,384]{1,0:T(8,128)(2,1)} %bitcast.3, bf16[2048,384]{1,0:T(8,128)(2,1)} %bitcast.4, bf16[384,2048]{1,0:T(8,128)(2,1)} %bitcast.5), custom_call_target="tpu_custom_call" | custom-call | tf_op jit(solution)/shard_map/layer/pallas_call | solution.py:474
  127.8 1.9 %copy.11 = bf16[128,2048]{1,0:T(8,128)(2,1)} copy(bf16[128,2048]{1,0:T(8,128)(2,1)} %layer.1) | data formatting | bytes 1048576
